TPU v7x, 32 devices: a whole 2x2x4 slice. The times are simulated.
32 devices in a mesh: dp: 4 (over y, x), vocab: 8 (over z, core).
Axes of the slice: x: 2, y: 2, z: 4, core: 2. Of those that a mesh axis runs over, the one named last changes fastest.
Arguments:
- hidden: bfloat16 [4, 32, 3584], P('dp', None, 'vocab'), may hold values from -6 to 6
- kl_hidden: bfloat16 [4, 32, 3584], P('dp', None, 'vocab'), may hold values from -6 to 6
- head_weight: bfloat16 [256000, 3584], P(('dp', 'vocab')), may hold values from -0.3125 to 0.3125
- labels: int32 [4, 32], P('dp'), may hold values from 0 to 255999
- token_mask: int32 [4, 32], P('dp'), may hold values 0 or 1
- kl_pair: int32 [4], P('dp'), may hold values from 0 to 3, as said below
- desirable: int32 [4], P('dp'), may hold values 0 or 1
- ref_logps: float32 [4, 64], P('dp', 'vocab'), may hold values from -23 to -11
Outputs:
- token_logps: float32 [4, 64], P('dp', 'vocab')
- seq_losses: float32 [4], P('dp')
- loss: float32 [], replicated
Inputs may be any that keep to these rules, and one draw needn't show every extreme that they name: kl_pair is a permutation of the 4 sequences with kl_pair[s] != s.
All inputs are finite; a program needn't handle non-finite values. No bound on the sum of `token_mask` or of `desirable` on one device may be relied on, other than what follows from the above.
Results may differ from a plain program's by a relative error of at most 0.0003.
Values may be sent and summed in bfloat16 or wider, within the bound.
A program may use at most 128 MiB of HBM per device.

v0:
```python
import jax
import jax.numpy as jnp
from jax import lax
from jax.sharding import PartitionSpec as P

kto_beta = 0.1
desirable_weight = 1.0
undesirable_weight = 1.33


def label_terms(logits, targets, first_row):
    shifted = targets - first_row
    inside = (shifted >= 0) & (shifted < logits.shape[1])
    clipped = jnp.clip(shifted, 0, logits.shape[1] - 1)
    picked = jnp.take_along_axis(logits, clipped[:, None], axis=1)[:, 0]
    return (jnp.sum(jnp.exp(logits), axis=1), jnp.where(inside, picked, 0.0))


def kto_losses(logratio, kl_total, seq_total, desirable):
    kl_estimate = kl_total / seq_total
    wanted = desirable_weight * (1.0 - jax.nn.sigmoid(kto_beta * (logratio - kl_estimate)))
    unwanted = undesirable_weight * (1.0 - jax.nn.sigmoid(kto_beta * (kl_estimate - logratio)))
    return jnp.where(desirable == 1, wanted, unwanted)


def on_device(hidden, kl_hidden, head_weight, labels, token_mask, kl_pair, desirable, ref_logps):
    sub_seq = hidden.shape[0]
    length = hidden.shape[1]
    vocab_rows = head_weight.shape[0]
    model_width = head_weight.shape[1]
    groups = lax.axis_size("vocab")
    vocab_index = lax.axis_index("vocab")
    data_index = lax.axis_index("dp")
    first_row = (data_index * groups + vocab_index) * vocab_rows
    all_labels, all_masks, all_pairs, all_desirable = (
        lax.all_gather(labels, "dp", axis=0, tiled=True),
        lax.all_gather(token_mask, "dp", axis=0, tiled=True),
        lax.all_gather(kl_pair, "dp", axis=0, tiled=True),
        lax.all_gather(desirable, "dp", axis=0, tiled=True),
    )
    targets = jnp.concatenate([all_labels, all_labels[all_pairs]], axis=1)
    weights_mask = jnp.concatenate([all_masks, all_masks[all_pairs]], axis=1).astype(jnp.float32)
    seq_total = targets.shape[0]
    columns = targets.shape[1]
    combined = jnp.concatenate([hidden, kl_hidden], axis=1)
    whole_rows = lax.all_gather(combined, "vocab", axis=2, tiled=True)
    portion = lax.all_gather(whole_rows, "dp", axis=0, tiled=True)
    number = portion.shape[0]
    logits = lax.dot_general(
        portion.reshape(number * columns, model_width),
        head_weight,
        (((1,), (1,)), ((), ())),
        preferred_element_type=jnp.float32,
    )
    portion_targets = targets.reshape(-1)
    part_sum, part_pick = label_terms(logits, portion_targets, first_row)
    token_stats = jnp.stack(
        [part_sum.reshape(number, columns), part_pick.reshape(number, columns)], axis=1
    )
    partition = token_stats[:, 0]
    picked = token_stats[:, 1]
    own_cols = columns // groups
    row_start = data_index * sub_seq
    col_start = vocab_index * own_cols
    ref_full = lax.dynamic_update_slice(
        jnp.zeros((seq_total, columns), jnp.float32), ref_logps, (row_start, col_start)
    )
    partition, picked, ref_all = lax.psum((partition, picked, ref_full), ("dp", "vocab"))
    token_logps = picked - jnp.log(partition)
    differences = weights_mask * (token_logps - ref_all)
    logratio = jnp.sum(differences[:, :length], axis=1)
    kl_terms = jnp.sum(differences[:, length:], axis=1)
    losses = kto_losses(logratio, jnp.sum(kl_terms), seq_total, all_desirable)
    own_logps = lax.dynamic_slice(token_logps, (row_start, col_start), (sub_seq, own_cols))
    own_losses = lax.dynamic_slice_in_dim(losses, row_start, sub_seq, 0)
    return (own_logps, own_losses, jnp.mean(losses))


def solution(mesh):
    in_specs = (
        P("dp", None, "vocab"),
        P("dp", None, "vocab"),
        P(("dp", "vocab"), None),
        P("dp", None),
        P("dp", None),
        P("dp"),
        P("dp"),
        P("dp", "vocab"),
    )
    out_specs = (P("dp", "vocab"), P("dp"), P())
    return jax.shard_map(
        on_device, mesh=mesh, in_specs=in_specs, out_specs=out_specs, check_vma=False
    )
```

profile of v0, /device:TPU:0, one launch (start us, length us, event | category | flops | bytes accessed | tf_op | source)
XLA Modules:
  0.0 153.6 jit_solution(2589287121122592298)
XLA Ops:
  7.2 0.0 all-gather.4.cloned.1.call-start
  7.2 0.8 pad_maximum_fusion
  8.0 0.2 copy.14
  8.2 23.7 %all_gather.20 = bf16[1,64,3584]{1,0,2:T(2,128)(2,1)S(1)} all-gather(bf16[1,64,448]{1,0,2:T(2,128)(2,1)S(1)} %copy.14), channel_id=1, replica_groups=mesh['dp'=4,'vocab'=8] {'vocab'}, dimensions={2}, use_global_device_ids=true | all-gather | bytes 516096 | tf_op jit(solution)/shard_map/all_gather | solution.py:46
  31.8 3.1 %copy.15 = bf16[1,64,3584]{2,1,0:T(8,128)(2,1)} copy(bf16[1,64,3584]{1,0,2:T(2,128)(2,1)S(1)} %all_gather.20) | data formatting | bytes 917504 | tf_op jit(solution)/shard_map/all_gather | solution.py:46
  34.9 0.0 all-gather.4.cloned.1.call-update
  36.2 1.2 dynamic-slice
  37.5 0.8 dynamic-update-slice
  38.3 0.8 dynamic-update-slice.1
  39.0 7.4 %all-reduce.2 = (s32[4]{0:T(128)S(1)}, s32[4]{0:T(128)S(1)}) all-reduce(s32[4]{0:T(128)S(1)} %dynamic-update-slice, s32[4]{0:T(128)S(1)} %dynamic-update-slice.1), channel_id=1, replica_groups=mesh['dp'=4,'vocab'=8] {'dp'}, use_global_device_ids=true, to_apply=%add | all-reduce | flops 8 | bytes 64
  46.4 7.9 %all-gather.1 = s32[4,1,32]{2,1,0:T(1,128)S(1)} all-gather(s32[1,1,32]{2,1,0:T(1,128)} %bitcast.17), channel_id=1, replica_groups=mesh['dp'=4,'vocab'=8] {'dp'}, dimensions={0}, use_global_device_ids=true | all-gather | bytes 640 | tf_op jit(solution)/shard_map/all_gather | solution.py:37
  54.3 0.6 gather_fusion.1
  54.9 7.2 %all-gather = s32[4,1,32]{2,1,0:T(1,128)S(1)} all-gather(s32[1,1,32]{2,1,0:T(1,128)} %bitcast.18), channel_id=1, replica_groups=mesh['dp'=4,'vocab'=8] {'dp'}, dimensions={0}, use_global_device_ids=true | all-gather | bytes 640 | tf_op jit(solution)/shard_map/all_gather | solution.py:36
  62.1 0.6 gather_fusion
  62.7 0.1 broadcast_clamp_fusion
  62.8 0.1 min.12
  62.8 0.8 dynamic_update_slice.3
  63.7 4.1 %all-gather.4.cloned.1.call-done = bf16[4,64,3584]{2,1,0:T(8,128)(2,1)} async-done(((bf16[1,64,3584]{2,1,0:T(8,128)(2,1)}), bf16[4,64,3584]{2,1,0:T(8,128)(2,1)}) %all-gather.4.cloned.1.call-update) | async-done | bytes 1835024 | tf_op jit(solution)/shard_map/all_gather | solution.py:47
  67.7 25.9 %exponential_reduce_fusion = (f32[256]{0:T(256)S(1)}, f32[256,8000]{0,1:T(8,128)}) fusion(bf16[256,3584]{1,0:T(8,128)(2,1)} %bitcast.19, bf16[8000,3584]{1,0:T(8,128)(2,1)} %param.10), kind=kOutput, calls=%fused_computation.3 | convolution fusion | flops 14682112000 | bytes 67372032 | tf_op jit(solution)/shard_map/dot_general | solution.py:49
  93.6 9.0 %gather_fusion.2 = f32[256]{0:T(256)S(1)} fusion(f32[256,8000]{0,1:T(8,128)} %get-tuple-element.15, s32[256]{0:T(256)S(1)} %bitcast.11), kind=kCustom, calls=%fused_computation.2 | custom fusion | bytes 4096 | tf_op jit(solution)/shard_map/jit(take_along_axis)/gather | solution.py:15
  102.6 0.1 gather.14
  102.7 0.1 select_select_fusion
  102.7 0.1 squeeze_stack_reshape.4
  102.8 38.9 %all-reduce.3 = (f32[4,64]{1,0:T(4,128)S(1)}, f32[4,64]{1,0:T(4,128)S(1)}, f32[4,64]{1,0:T(4,128)S(1)}) all-reduce(f32[4,64]{1,0:T(4,128)S(1)} %select_select_fusion, f32[4,64]{1,0:T(4,128)S(1)} %squeeze_stack_reshape.4, f32[4,64]{1,0:T(4,128)S(1)} %dynamic_update_slice.3), channel_id=1, replica_groups=mesh['dp'=4,'vocab'=8] {'dp','vocab'}, use_global_device_ids=true, to_apply=%region_0.1 | all-reduce | flops 768 | bytes 6144 | tf_op jit(solution)/shard_map/psum | solution.py:68
  141.8 0.1 fusion
  141.8 0.6 dynamic_slice.6
  142.4 0.7 slice_reduce_fusion
  143.7 0.6 fusion.4
  144.4 0.6 dynamic_slice.7
  (9 shorter events, 0.0 us)
Async XLA Ops:
  7.2 60.6 %all-gather.4.cloned.1.call-start = ((), (), s32[]{:S(2)}) async-start(), calls=%async_computation | async-start | bytes 2293760 | tf_op jit(solution)/shard_map/all_gather | solution.py:47
Sparse Core Ops, SparseCore 0:
  35.1 32.6 all-gather.3
where the time goes:
time: 154 us
  blocking collectives  85.1 us (55%)
  matrix products  25.9 us (17%)
  local copies, waits for them, and re-layouts  18.3 us (12%)
  between operations  17.8 us (12%)
  waiting for transfers between devices  4.07 us (3%)
  other arithmetic  2.34 us (2%)
    psum x1, blocking collectives, on_device(): lax.psum((partition, picked, ref_full), ('dp', 'vocab'))  38.9 us
    dot_general x1, matrix products, on_device(): lax.dot_general(portion.reshape(number * columns, model_width), head_weig...  25.9 us
    all_gather x1, blocking collectives, on_device(): whole_rows = lax.all_gather(combined, 'vocab', axis=2, tiled=True)  23.7 us
    gather x2, local copies, waits for them, and re-layouts, label_terms(): picked = jnp.take_along_axis(logits, clipped[:, None], axis=1)[:, 0]  9.07 us
    all_gather x1, blocking collectives, on_device(): lax.all_gather(token_mask, 'dp', axis=0, tiled=True)  7.92 us
    unnamed x1, blocking collectives  7.39 us
    all_gather x1, blocking collectives, on_device(): lax.all_gather(labels, 'dp', axis=0, tiled=True)  7.23 us
    all_gather x1, waiting for transfers between devices, on_device(): portion = lax.all_gather(whole_rows, 'dp', axis=0, tiled=True)  4.05 us
  transfers between devices with their start and end apart: 1, of which 1 were waited for; matrix products, arithmetic and copies ran while one was open for 3% of the time, Pallas kernels for 0%

commit v1 on v0

--- a/solution.py
+++ b/solution.py
@@ -43,7 +43,7 @@
     seq_total = targets.shape[0]
     columns = targets.shape[1]
     combined = jnp.concatenate([hidden, kl_hidden], axis=1)
-    whole_rows = lax.all_gather(combined, "vocab", axis=2, tiled=True)
+    whole_rows = jnp.concatenate(lax.all_gather(combined, "vocab"), axis=2)
     portion = lax.all_gather(whole_rows, "dp", axis=0, tiled=True)
     number = portion.shape[0]
     logits = lax.dot_general(

time: 154 us -> 147 us (0.955)
  blocking collectives: 85.1 us -> 78 us
  local copies, waits for them, and re-layouts: 18.3 us -> 16.7 us
    all_gather x1, blocking collectives: 23.7 us -> 16.5 us  [on_device(): whole_rows = jnp.concatenate(lax.all_gather(combined, 'vocab'), axis=2)]
    all_gather x1 -> x0, local copies, waits for them, and re-layouts: 3.09 us -> none  [on_device(): whole_rows = lax.all_gather(combined, 'vocab', axis=2, tiled=True)]
    reshape x0 -> x2, local copies, waits for them, and re-layouts: none -> 1.62 us  [on_device(): whole_rows = jnp.concatenate(lax.all_gather(combined, 'vocab'), axis=2)]
where the time goes in v1:
time: 147 us; the launch traced here: 146 us
  blocking collectives  78 us (53%)
  matrix products  25.8 us (18%)
  between operations  17.8 us (12%)
  local copies, waits for them, and re-layouts  16.7 us (11%)
  waiting for transfers between devices  5.58 us (4%)
  other arithmetic  2.34 us (2%)
    psum x1, blocking collectives, on_device(): lax.psum((partition, picked, ref_full), ('dp', 'vocab'))  39 us
    dot_general x1, matrix products, on_device(): lax.dot_general(portion.reshape(number * columns, model_width), head_weig...  25.8 us
    all_gather x1, blocking collectives, on_device(): whole_rows = jnp.concatenate(lax.all_gather(combined, 'vocab'), axis=2)  16.5 us
    gather x2, local copies, waits for them, and re-layouts, label_terms(): picked = jnp.take_along_axis(logits, clipped[:, None], axis=1)[:, 0]  9.07 us
    all_gather x1, blocking collectives, on_device(): lax.all_gather(token_mask, 'dp', axis=0, tiled=True)  7.98 us
    unnamed x1, blocking collectives  7.37 us
    all_gather x1, blocking collectives, on_device(): lax.all_gather(labels, 'dp', axis=0, tiled=True)  7.17 us
    all_gather x1, waiting for transfers between devices, on_device(): portion = lax.all_gather(whole_rows, 'dp', axis=0, tiled=True)  5.57 us
  transfers between devices with their start and end apart: 1, of which 1 were waited for; matrix products, arithmetic and copies ran while one was open for 3% of the time, Pallas kernels for 0%

profile of v1, /device:TPU:0, one launch (start us, length us, event | category | flops | bytes accessed | tf_op | source)
XLA Modules:
  0.0 146.3 jit_solution(12750053764799776210)
XLA Ops:
  7.2 0.0 all-gather.5.cloned.1.call-start
  7.2 0.8 pad_maximum_fusion
  8.0 16.5 %all-gather = bf16[8,64,448]{2,1,0:T(8,128)(2,1)S(1)} all-gather(bf16[1,64,448]{2,1,0:T(8,128)(2,1)S(1)} %pad_maximum_fusion), channel_id=2, replica_groups=mesh['dp'=4,'vocab'=8] {'vocab'}, dimensions={0}, use_global_device_ids=true | all-gather | bytes 516096 | tf_op jit(solution)/shard_map/all_gather | solution.py:46
  24.5 0.3 copy.12
  24.8 1.3 reshape.71
  26.1 0.0 all-gather.5.cloned.1.call-update
  27.4 1.2 dynamic-slice
  28.7 0.8 dynamic-update-slice
  29.4 0.8 dynamic-update-slice.1
  30.2 7.4 %all-reduce.2 = (s32[4]{0:T(128)S(1)}, s32[4]{0:T(128)S(1)}) all-reduce(s32[4]{0:T(128)S(1)} %dynamic-update-slice, s32[4]{0:T(128)S(1)} %dynamic-update-slice.1), channel_id=1, replica_groups=mesh['dp'=4,'vocab'=8] {'dp'}, use_global_device_ids=true, to_apply=%add | all-reduce | flops 8 | bytes 64
  37.6 8.0 %all-gather.2 = s32[4,1,32]{2,1,0:T(1,128)S(1)} all-gather(s32[1,1,32]{2,1,0:T(1,128)} %bitcast.23), channel_id=1, replica_groups=mesh['dp'=4,'vocab'=8] {'dp'}, dimensions={0}, use_global_device_ids=true | all-gather | bytes 640 | tf_op jit(solution)/shard_map/all_gather | solution.py:37
  45.6 0.6 gather_fusion.1
  46.1 7.2 %all-gather.1 = s32[4,1,32]{2,1,0:T(1,128)S(1)} all-gather(s32[1,1,32]{2,1,0:T(1,128)} %bitcast.24), channel_id=1, replica_groups=mesh['dp'=4,'vocab'=8] {'dp'}, dimensions={0}, use_global_device_ids=true | all-gather | bytes 640 | tf_op jit(solution)/shard_map/all_gather | solution.py:36
  53.3 0.6 gather_fusion
  53.9 0.1 broadcast_clamp_fusion
  53.9 0.1 min.12
  54.0 0.8 dynamic_update_slice.3
  54.8 5.6 %all-gather.5.cloned.1.call-done = bf16[4,64,3584]{2,1,0:T(8,128)(2,1)} async-done(((bf16[1,64,3584]{2,1,0:T(8,128)(2,1)}), bf16[4,64,3584]{2,1,0:T(8,128)(2,1)}) %all-gather.5.cloned.1.call-update) | async-done | bytes 1835024 | tf_op jit(solution)/shard_map/all_gather | solution.py:47
  60.4 25.8 %exponential_reduce_fusion = (f32[256]{0:T(256)S(1)}, f32[256,8000]{0,1:T(8,128)}) fusion(bf16[256,3584]{1,0:T(8,128)(2,1)} %bitcast.25, bf16[8000,3584]{1,0:T(8,128)(2,1)} %param.10), kind=kOutput, calls=%fused_computation.3 | convolution fusion | flops 14682112000 | bytes 67372032 | tf_op jit(solution)/shard_map/dot_general | solution.py:49
  86.3 9.0 %gather_fusion.2 = f32[256]{0:T(256)S(1)} fusion(f32[256,8000]{0,1:T(8,128)} %get-tuple-element.15, s32[256]{0:T(256)S(1)} %bitcast.16), kind=kCustom, calls=%fused_computation.2 | custom fusion | bytes 4096 | tf_op jit(solution)/shard_map/jit(take_along_axis)/gather | solution.py:15
  95.3 0.1 gather.14
  95.3 0.1 select_select_fusion
  95.4 0.1 squeeze_stack_reshape.4
  95.5 39.0 %all-reduce.3 = (f32[4,64]{1,0:T(4,128)S(1)}, f32[4,64]{1,0:T(4,128)S(1)}, f32[4,64]{1,0:T(4,128)S(1)}) all-reduce(f32[4,64]{1,0:T(4,128)S(1)} %select_select_fusion, f32[4,64]{1,0:T(4,128)S(1)} %squeeze_stack_reshape.4, f32[4,64]{1,0:T(4,128)S(1)} %dynamic_update_slice.3), channel_id=1, replica_groups=mesh['dp'=4,'vocab'=8] {'dp','vocab'}, use_global_device_ids=true, to_apply=%region_0.1 | all-reduce | flops 768 | bytes 6144 | tf_op jit(solution)/shard_map/psum | solution.py:68
  134.5 0.1 fusion
  134.6 0.6 dynamic_slice.6
  135.1 0.7 slice_reduce_fusion
  136.5 0.6 fusion.4
  137.1 0.6 dynamic_slice.7
  (9 shorter events, 0.0 us)
Async XLA Ops:
  7.2 53.2 %all-gather.5.cloned.1.call-start = ((), (), s32[]{:S(2)}) async-start(), calls=%async_computation | async-start | bytes 2293760 | tf_op jit(solution)/shard_map/all_gather | solution.py:47
Sparse Core Ops, SparseCore 0:
  26.3 34.0 all-gather.4
